TPU v7x, 128 devices: a whole 4x4x4 slice. The times are simulated.
128 devices in a mesh: dp: 8 (over z, core), mp: 16 (over y, x).
Axes of the slice: x: 4, y: 4, z: 4, core: 2. Of those that a mesh axis runs over, the one named last changes fastest.
Arguments:
- crop_hidden: bfloat16 [8, 1536, 8192], P(None, 'dp', 'mp'), may hold values from -15 to 15
- projector_weight: bfloat16 [8192, 8192], P('mp'), may hold values from -0.21213203 to 0.21213203
- pairing: int32 [8, 1536], P(None, 'dp'), may hold values from 0 to 191, as said below
Outputs:
- embeddings: float32 [8192, 8, 1536], P('mp', 'dp')
- loss_terms: float32 [4], replicated
Inputs may be any that keep to these rules, and one draw needn't show every extreme that they name: Each aligned block of 192 entries of a row of pairing is a permutation of 0 to 191.
All inputs are finite; a program needn't handle non-finite values.
Results may differ from a plain program's by a relative error of at most 0.0003.
Values may be sent and summed in bfloat16 or wider, within the bound.
No kernel may reach another device: no remote copies, remote signals or barrier semaphores. Data moves between devices by JAX's collectives and lax.ppermute only.
A program may use at most 128 MiB of HBM per device.

v0:
```python
import functools
import jax
import jax.numpy as jnp
from jax import lax
from jax.sharding import Mesh
from jax.sharding import PartitionSpec as P

MP = ("mp_0", "mp_1")
DP = ("dp_0", "dp_1")
DP_MP = ("dp_0", "dp_1", "mp_0", "mp_1")
highest = lax.Precision.HIGHEST
epsilon = 0.0001


def by_axis(x, axes):
    return functools.reduce(lax.psum, axes, x)


def local(crop_hidden, projector_weight, pairing):
    crop_count, local_rows, width_part = crop_hidden.shape
    features = projector_weight.shape[1]
    total_rows = crop_count * local_rows
    column_block = lax.all_to_all(projector_weight, MP, split_axis=1, concat_axis=0, tiled=True)
    shards = lax.all_gather(crop_hidden, MP, axis=2, tiled=True)
    flat_piece = shards.reshape(total_rows, shards.shape[2])
    embedded = lax.dot_general(
        column_block, flat_piece, (((0,), (1,)), ((), ())), preferred_element_type=jnp.float32
    )
    feature_part = embedded.shape[0]
    by_crop = embedded.reshape(feature_part, crop_count, local_rows)
    onehot = (pairing[:, :, None] == jnp.arange(local_rows, dtype=jnp.int32)[None, None, :]).astype(
        jnp.float32
    )
    aligned = jnp.einsum("jcr,cri->jci", by_crop, onehot, precision=highest)
    invariance = 0.0
    for anchor in range(2):
        differ = aligned - aligned[:, anchor : anchor + 1, :]
        invariance = invariance + jnp.sum(differ * differ)
    owned_block = lax.all_to_all(by_crop, DP, split_axis=1, concat_axis=2, tiled=True)
    batch_rows = owned_block.shape[2]
    column_mean = jnp.mean(owned_block, axis=2, keepdims=True)
    centered = owned_block - column_mean
    variance = jnp.sum(centered * centered, axis=2) / (batch_rows - 1)
    hinge_sum = jnp.sum(jax.nn.relu(1.0 - jnp.sqrt(variance + epsilon)))
    diagonal_sq = jnp.sum(variance * variance)
    gram_scale = 1.0 / ((batch_rows - 1) * (batch_rows - 1))
    partial_gram = jnp.einsum("jcr,jcs->crs", centered, centered, precision=highest)
    gram_block = lax.psum(partial_gram.astype(jnp.bfloat16), MP).astype(jnp.float32)
    frobenius = jnp.where(
        lax.axis_index(MP) == 0, jnp.sum(gram_block * gram_block) * gram_scale, 0.0
    )
    totals = (
        by_axis(invariance, DP_MP),
        by_axis(hinge_sum, DP_MP),
        by_axis(frobenius - diagonal_sq, DP_MP),
    )
    invariance_loss = totals[0] / (2 * (crop_count - 1) * batch_rows * features)
    variance_loss = totals[1] / (crop_count * features)
    covariance_loss = totals[2] / (crop_count * features)
    total_loss = 25.0 * invariance_loss + 25.0 * variance_loss + covariance_loss
    loss_terms = jnp.stack([invariance_loss, variance_loss, covariance_loss, total_loss])
    return (owned_block, loss_terms)


def solution(mesh):
    torus = Mesh(mesh.devices.reshape(4, 2, 4, 4), ("dp_0", "dp_1", "mp_0", "mp_1"))
    placed = (P(None, DP, MP), P(MP, None), P(None, DP))
    return jax.shard_map(
        local, mesh=torus, in_specs=placed, out_specs=(P(MP, DP, None), P()), check_vma=False
    )
```

profile of v0, /device:TPU:0, one launch (start us, length us, event | category | flops | bytes accessed | tf_op | source)
XLA Modules:
  0.0 498.9 jit_solution(17605152332946094416)
XLA Ops:
  7.2 0.0 all-gather.2.cloned.1.call-start
  7.2 0.7 all-gather.2.cloned.1.call-update
  7.9 0.0 all-reduce.6.cloned.1.call-start
  7.9 7.5 %copy.9 = bf16[64,16,8,512]{3,2,0,1:T(8,128)(2,1)} copy(bf16[64,16,8,512]{3,2,1,0:T(8,128)(2,1)} %bitcast.30) | data formatting | bytes 16777216 | tf_op jit(solution)/shard_map/all_to_all | solution.py:23
  15.4 128.3 %all_to_all.31 = bf16[512,16,512]{2,0,1:T(8,128)(2,1)} all-to-all(bf16[512,16,512]{2,0,1:T(8,128)(2,1)} %bitcast.29), channel_id=1, replica_groups=mesh['dp_0'=4,'dp_1'=2,'mp_0'=4,'mp_1'=4] {'mp_0','mp_1'}, dimensions={1} | all-to-all | bytes 16777216 | tf_op jit(solution)/shard_map/all_to_all | solution.py:23
  143.8 117.0 %all-gather.2.cloned.1.call-done = bf16[8,192,8192]{2,1,0:T(8,128)(2,1)} async-done(((bf16[8,192,512]{2,1,0:T(8,128)(2,1)}), bf16[8,192,8192]{2,1,0:T(8,128)(2,1)}) %all-gather.2.cloned.1.call-update) | async-done | bytes 25165840 | tf_op jit(solution)/shard_map/all_gather | solution.py:24
  260.8 18.9 %fusion.2 = f32[512,8,192]{0,2,1:T(8,128)S(1)} fusion(bf16[8192,512,1]{1,0,2:T(8,128)(2,1)} %bitcast.31, bf16[8,192,8192]{2,1,0:T(8,128)(2,1)} %all-gather.2.cloned.1.call-done), kind=kOutput, calls=%fused_computation.17 | convolution fusion | flops 12884901888 | bytes 36700160 | tf_op jit(solution)/shard_map/dot_general | solution.py:26
  279.7 0.0 copy-start
  279.7 1.7 copy-done
  281.3 42.7 %all_to_all.32 = f32[512,8,192]{0,2,1:T(8,128)S(1)} all-to-all(f32[512,8,192]{0,2,1:T(8,128)S(1)} %fusion.2), channel_id=1, replica_groups=mesh['dp_0'=4,'dp_1'=2,'mp_0'=4,'mp_1'=4] {'dp_0','dp_1'}, dimensions={1} | all-to-all | bytes 6291456 | tf_op jit(solution)/shard_map/all_to_all | solution.py:39
  324.0 0.3 reduce_sum.65
  324.3 0.6 multiply_reduce_fusion.1
  324.8 16.8 %fusion = bf16[1,1536,1536]{2,1,0:T(8,128)(2,1)} fusion(f32[512,1536]{0,1:T(8,128)S(1)} %bitcast.32), kind=kOutput, calls=%fused_computation.3 | convolution fusion | flops 14497873920 | bytes 7864320 | tf_op jit(solution)/shard_map/jcr,jcs->crs/dot_general | solution.py:47
  341.6 0.0 copy-start.1
  341.6 0.0 all-reduce.6.cloned.1.call-update
  341.6 0.7 copy-done.1
  342.3 3.9 convolution_bitcast_fusion
  346.2 0.1 slice_bitcast_fusion.1
  346.2 2.0 multiply_reduce_fusion.2
  349.5 5.4 %copy.6 = f32[512,1,1536]{2,1,0:T(1,128)} copy(f32[512,1,1536]{0,2,1:T(8,128)S(1)} %bitcast.28) | data formatting | bytes 6291456
  354.9 0.7 multiply_reduce_fusion.4
  355.6 91.4 %all-reduce.6.cloned.1.call-done = bf16[1,1536,1536]{2,1,0:T(8,128)(2,1)} async-done(((bf16[1,1536,1536]{2,1,0:T(8,128)(2,1)}), bf16[1,1536,1536]{2,1,0:T(8,128)(2,1)}) %all-reduce.6.cloned.1.call-update) | async-done | bytes 4718608 | tf_op jit(solution)/shard_map/psum | solution.py:48
  447.0 5.3 %multiply_reduce_fusion = f32[]{:T(128)} fusion(bf16[1,1536,1536]{2,1,0:T(8,128)(2,1)} %all-reduce.6.cloned.1.call-done), kind=kLoop, calls=%fused_computation | loop fusion | flops 7077887 | bytes 4718596 | tf_op jit(solution)/shard_map/reduce_sum | solution.py:50
  453.5 11.3 %all-reduce.2 = (f32[]{:T(128)}, f32[]{:T(128)}, f32[]{:T(128)}) all-reduce(f32[]{:T(128)S(6)} %add.47, f32[]{:T(128)} %get-tuple-element.7, f32[]{:T(128)S(6)} %sub.61), channel_id=1, replica_groups=mesh['dp_0'=4,'dp_1'=2,'mp_0'=4,'mp_1'=4] {'dp_0'}, use_global_device_ids=true, to_apply=%region_2.0 | all-reduce | flops 3 | bytes 24 | tf_op jit(solution)/shard_map/psum | solution.py:16
  464.8 3.2 all-reduce.3
  467.9 11.0 %all-reduce.1 = (f32[]{:T(128)}, f32[]{:T(128)}, f32[]{:T(128)}) all-reduce(f32[]{:T(128)} %get-tuple-element.17, f32[]{:T(128)} %get-tuple-element.18, f32[]{:T(128)} %get-tuple-element.19), channel_id=1, replica_groups=mesh['dp_0'=4,'dp_1'=2,'mp_0'=4,'mp_1'=4] {'mp_0'}, use_global_device_ids=true, to_apply=%region_4.5 | all-reduce | flops 3 | bytes 24 | tf_op jit(solution)/shard_map/psum | solution.py:16
  478.9 9.4 %all-reduce = (f32[]{:T(128)}, f32[]{:T(128)}, f32[]{:T(128)}) all-reduce(f32[]{:T(128)} %get-tuple-element.11, f32[]{:T(128)} %get-tuple-element.12, f32[]{:T(128)} %get-tuple-element.13), channel_id=1, replica_groups=mesh['dp_0'=4,'dp_1'=2,'mp_0'=4,'mp_1'=4] {'mp_1'}, use_global_device_ids=true, to_apply=%region_5.6 | all-reduce | flops 3 | bytes 24 | tf_op jit(solution)/shard_map/psum | solution.py:16
  491.5 0.6 pad_maximum_fusion
  (1 shorter events, 0.0 us)
Async XLA Ops:
  7.2 253.6 %all-gather.2.cloned.1.call-start = ((), (), s32[]{:S(2)}) async-start(), calls=%async_computation.2 | async-start | bytes 26738688 | tf_op jit(solution)/shard_map/all_gather | solution.py:24
  7.9 439.1 %all-reduce.6.cloned.1.call-start = ((), (), s32[]{:S(2)}) async-start(), calls=%async_computation.3 | async-start | bytes 9437184 | tf_op jit(solution)/shard_map/psum | solution.py:48
  279.7 1.7 copy-start
  341.6 0.7 copy-start.1
Sparse Core Ops, SparseCore 0:
  10.1 250.6 all-gather.1
  341.7 105.2 all-reduce.5
where the time goes:
time: 499 us
  waiting for transfers between devices  209 us (42%)
  blocking collectives  206 us (41%)
  matrix products  39.5 us (8%)
  between operations  19.8 us (4%)
  local copies, waits for them, and re-layouts  15.3 us (3%)
  other arithmetic  9.4 us (2%)
    all_to_all x1, blocking collectives, local(): lax.all_to_all(projector_weight, MP, split_axis=1, concat_axis=0, tiled=T...  128 us
    all_gather x1, waiting for transfers between devices, local(): shards = lax.all_gather(crop_hidden, MP, axis=2, tiled=True)  117 us
    psum x1, waiting for transfers between devices, local(): lax.psum(partial_gram.astype(jnp.bfloat16), MP).astype(jnp.float32)  91.4 us
    all_to_all x1, blocking collectives, local(): lax.all_to_all(by_crop, DP, split_axis=1, concat_axis=2, tiled=True)  42.7 us
    psum x4, blocking collectives, by_axis(): return functools.reduce(lax.psum, axes, x)  34.8 us
    dot_general x1, matrix products, local(): lax.dot_general(column_block, flat_piece, (((0,), (1,)), ((), ())), prefe...  18.9 us
    dot_general x1, matrix products, local(): jnp.einsum('jcr,jcs->crs', centered, centered, precision=highest)  16.8 us
  transfers between devices with their start and end apart: 2, of which 2 were waited for; matrix products, arithmetic and copies ran while one was open for 4% of the time, Pallas kernels for 0%

commit v1 on v0

--- a/solution.py
+++ b/solution.py
@@ -45,7 +45,9 @@
     diagonal_sq = jnp.sum(variance * variance)
     gram_scale = 1.0 / ((batch_rows - 1) * (batch_rows - 1))
     partial_gram = jnp.einsum("jcr,jcs->crs", centered, centered, precision=highest)
-    gram_block = lax.psum(partial_gram.astype(jnp.bfloat16), MP).astype(jnp.float32)
+    gram_block = jnp.sum(lax.all_gather(partial_gram.astype(jnp.bfloat16), MP), axis=0).astype(
+        jnp.float32
+    )
     frobenius = jnp.where(
         lax.axis_index(MP) == 0, jnp.sum(gram_block * gram_block) * gram_scale, 0.0
     )

time: 499 us -> 830 us (1.66)
  waiting for transfers between devices: 209 us -> 512 us
  other arithmetic: 9.4 us -> 36.5 us
    all_gather x0 -> x1, waiting for transfers between devices: none -> 395 us  [local(): lax.all_gather(partial_gram.astype(jnp.bfloat16), MP)]
    psum x1 -> x0, waiting for transfers between devices: 91.4 us -> none  [local(): lax.psum(partial_gram.astype(jnp.bfloat16), MP).astype(jnp.float32)]
    reduce_sum x0 -> x1, other arithmetic: none -> 26.9 us  [local(): jnp.sum(lax.all_gather(partial_gram.astype(jnp.bfloat16), MP), axis=0)]
  transfers between devices with their start and end apart: 2 -> 2, of which waited for: 2 -> 2; matrix products, arithmetic and copies ran while one was open for 4% -> 2% of each run, Pallas kernels for 0% -> 0%
where the time goes in v1:
time: 830 us
  waiting for transfers between devices  512 us (62%)
  blocking collectives  206 us (25%)
  matrix products  39.6 us (5%)
  other arithmetic  36.5 us (4%)
  between operations  20 us (2%)
  local copies, waits for them, and re-layouts  15.3 us (2%)
    all_gather x1, waiting for transfers between devices, local(): lax.all_gather(partial_gram.astype(jnp.bfloat16), MP)  395 us
    all_to_all x1, blocking collectives, local(): lax.all_to_all(projector_weight, MP, split_axis=1, concat_axis=0, tiled=T...  128 us
    all_gather x1, waiting for transfers between devices, local(): shards = lax.all_gather(crop_hidden, MP, axis=2, tiled=True)  117 us
    all_to_all x1, blocking collectives, local(): lax.all_to_all(by_crop, DP, split_axis=1, concat_axis=2, tiled=True)  42.7 us
    psum x4, blocking collectives, by_axis(): return functools.reduce(lax.psum, axes, x)  34.8 us
    reduce_sum x1, other arithmetic, local(): jnp.sum(lax.all_gather(partial_gram.astype(jnp.bfloat16), MP), axis=0)  26.9 us
    dot_general x1, matrix products, local(): lax.dot_general(column_block, flat_piece, (((0,), (1,)), ((), ())), prefe...  18.9 us
    dot_general x1, matrix products, local(): jnp.einsum('jcr,jcs->crs', centered, centered, precision=highest)  16.9 us
  transfers between devices with their start and end apart: 2, of which 2 were waited for; matrix products, arithmetic and copies ran while one was open for 2% of the time, Pallas kernels for 0%

profile of v1, /device:TPU:0, one launch (start us, length us, event | category | flops | bytes accessed | tf_op | source)
XLA Modules:
  0.0 829.6 jit_solution(14947903450264423572)
XLA Ops:
  7.2 0.0 all-gather.4.cloned.1.call-start
  7.2 0.7 all-gather.4.cloned.1.call-update
  7.9 0.0 all-gather.6.cloned.1.call-start
  7.9 7.5 copy.11
  15.4 128.3 %all_to_all.31 = bf16[512,16,512]{2,0,1:T(8,128)(2,1)} all-to-all(bf16[512,16,512]{2,0,1:T(8,128)(2,1)} %bitcast.28), channel_id=1, replica_groups=mesh['dp_0'=4,'dp_1'=2,'mp_0'=4,'mp_1'=4] {'mp_0','mp_1'}, dimensions={1} | all-to-all | bytes 16777216 | tf_op jit(solution)/shard_map/all_to_all | solution.py:23
  143.8 117.0 %all-gather.4.cloned.1.call-done = bf16[8,192,8192]{2,1,0:T(8,128)(2,1)} async-done(((bf16[8,192,512]{2,1,0:T(8,128)(2,1)}), bf16[8,192,8192]{2,1,0:T(8,128)(2,1)}) %all-gather.4.cloned.1.call-update) | async-done | bytes 25165840 | tf_op jit(solution)/shard_map/all_gather | solution.py:24
  260.8 18.9 %fusion.1 = f32[512,8,192]{0,2,1:T(8,128)S(1)} fusion(bf16[8192,512,1]{1,0,2:T(8,128)(2,1)} %bitcast.30, bf16[8,192,8192]{2,1,0:T(8,128)(2,1)} %all-gather.4.cloned.1.call-done), kind=kOutput, calls=%fused_computation.16 | convolution fusion | flops 12884901888 | bytes 36700160 | tf_op jit(solution)/shard_map/dot_general | solution.py:26
  279.7 0.0 copy-start
  279.7 1.7 copy-done
  281.3 42.7 %all_to_all.32 = f32[512,8,192]{0,2,1:T(8,128)S(1)} all-to-all(f32[512,8,192]{0,2,1:T(8,128)S(1)} %fusion.1), channel_id=1, replica_groups=mesh['dp_0'=4,'dp_1'=2,'mp_0'=4,'mp_1'=4] {'dp_0','dp_1'}, dimensions={1} | all-to-all | bytes 6291456 | tf_op jit(solution)/shard_map/all_to_all | solution.py:39
  324.0 0.3 reduce_sum.77
  324.3 0.6 multiply_reduce_fusion.1
  324.8 16.9 %convolution_convert_fusion = bf16[1536,1536]{1,0:T(8,128)(2,1)} fusion(f32[512,1536]{0,1:T(8,128)S(1)} %bitcast.31), kind=kOutput, calls=%fused_computation.2 | convolution fusion | flops 14497873920 | bytes 7864320 | tf_op jit(solution)/shard_map/jcr,jcs->crs/dot_general | solution.py:47
  341.7 0.0 copy-start.1
  341.7 0.0 all-gather.6.cloned.1.call-update
  341.7 0.7 copy-done.1
  342.4 3.9 convolution_bitcast_fusion
  346.3 0.1 slice_bitcast_fusion.1
  346.3 2.0 multiply_reduce_fusion.2
  349.6 5.4 copy.8
  355.1 0.7 multiply_reduce_fusion.4
  355.7 394.6 %all-gather.6.cloned.1.call-done = bf16[24576,1536]{1,0:T(8,128)(2,1)} async-done(((bf16[1536,1536]{1,0:T(8,128)(2,1)}), bf16[24576,1536]{1,0:T(8,128)(2,1)}) %all-gather.6.cloned.1.call-update) | async-done | bytes 75497488 | tf_op jit(solution)/shard_map/all_gather | solution.py:48
  750.3 26.9 %reduce.8 = bf16[1536,1536]{1,0:T(8,128)(2,1)} reduce(bf16[16,1536,1536]{2,1,0:T(8,128)(2,1)} %bitcast.10, bf16[]{:T(256)} %constant.37.clone.1), dimensions={0}, to_apply=%region_13.14 | reduce | flops 35389440 | bytes 80216064 | tf_op jit(solution)/shard_map/reduce_sum | solution.py:48
  777.3 5.4 multiply_reduce_fusion
  784.1 11.3 %all-reduce.2 = (f32[]{:T(128)}, f32[]{:T(128)}, f32[]{:T(128)}) all-reduce(f32[]{:T(128)S(6)} %add.45, f32[]{:T(128)} %get-tuple-element.9, f32[]{:T(128)S(6)} %sub.61), channel_id=1, replica_groups=mesh['dp_0'=4,'dp_1'=2,'mp_0'=4,'mp_1'=4] {'dp_0'}, use_global_device_ids=true, to_apply=%region_2.0 | all-reduce | flops 3 | bytes 24 | tf_op jit(solution)/shard_map/psum | solution.py:16
  795.3 3.2 all-reduce.3
  798.5 11.1 %all-reduce.1 = (f32[]{:T(128)}, f32[]{:T(128)}, f32[]{:T(128)}) all-reduce(f32[]{:T(128)} %get-tuple-element.19, f32[]{:T(128)} %get-tuple-element.20, f32[]{:T(128)} %get-tuple-element.21), channel_id=1, replica_groups=mesh['dp_0'=4,'dp_1'=2,'mp_0'=4,'mp_1'=4] {'mp_0'}, use_global_device_ids=true, to_apply=%region_4.5 | all-reduce | flops 3 | bytes 24 | tf_op jit(solution)/shard_map/psum | solution.py:16
  809.6 9.3 %all-reduce = (f32[]{:T(128)}, f32[]{:T(128)}, f32[]{:T(128)}) all-reduce(f32[]{:T(128)} %get-tuple-element.13, f32[]{:T(128)} %get-tuple-element.14, f32[]{:T(128)} %get-tuple-element.15), channel_id=1, replica_groups=mesh['dp_0'=4,'dp_1'=2,'mp_0'=4,'mp_1'=4] {'mp_1'}, use_global_device_ids=true, to_apply=%region_5.6 | all-reduce | flops 3 | bytes 24 | tf_op jit(solution)/shard_map/psum | solution.py:16
  822.1 0.6 pad_maximum_fusion
  (1 shorter events, 0.0 us)
Async XLA Ops:
  7.2 253.6 %all-gather.4.cloned.1.call-start = ((), (), s32[]{:S(2)}) async-start(), calls=%async_computation.2 | async-start | bytes 26738688 | tf_op jit(solution)/shard_map/all_gather | solution.py:24
  7.9 742.4 %all-gather.6.cloned.1.call-start = ((), (), s32[]{:S(2)}) async-start(), calls=%async_computation.3 | async-start | bytes 80216064 | tf_op jit(solution)/shard_map/all_gather | solution.py:48
  279.7 1.7 copy-start
  341.7 0.7 copy-start.1
Sparse Core Ops, SparseCore 0:
  10.1 250.6 all-gather.3
  341.8 408.4 all-gather.5
